TPU v7x, 32 devices: a whole 2x2x4 slice. The times are simulated.
32 devices in a mesh: ey: 4 (over z), ex: 8 (over y, x, core).
Axes of the slice: x: 2, y: 2, z: 4, core: 2. Of those that a mesh axis runs over, the one named last changes fastest.
Arguments:
- x: bfloat16 [2048, 2048], P(('ey', 'ex'))
- kv_k: bfloat16 [2048, 256, 1, 128], P(('ey', 'ex'))
- kv_v: bfloat16 [2048, 256, 1, 128], P(('ey', 'ex'))
- lens: int32 [2048], P(('ey', 'ex'))
- topk_idx: int32 [2048, 6], P(('ey', 'ex'))
- gates: float32 [2048, 6], P(('ey', 'ex'))
- ln1: bfloat16 [2048], replicated
- ln2: bfloat16 [2048], replicated
- wq: bfloat16 [2048, 2048], replicated
- wo: bfloat16 [2048, 2048], replicated
- ws1: bfloat16 [2048, 1408], replicated
- ws3: bfloat16 [2048, 1408], replicated
- ws2: bfloat16 [1408, 2048], replicated
- w1: bfloat16 [64, 2048, 1408], P(('ey', 'ex'))
- w3: bfloat16 [64, 2048, 1408], P(('ey', 'ex'))
- w2: bfloat16 [64, 1408, 2048], P(('ey', 'ex'))
Outputs:
- output: bfloat16 [2048, 2048], P(('ey', 'ex'))
All inputs are finite; a program needn't handle non-finite values.
Results may differ from a plain program's by a relative error of at most 0.0123182.
Values are sent between devices in bfloat16 or wider.
A program may use at most 1 GiB of HBM per device.

v0:
```python
import jax
import jax.numpy as jnp
from jax import lax
from jax.sharding import PartitionSpec as P

EPS = 1e-6
BF = jnp.bfloat16
F32 = jnp.float32


def _rms(v, w):
    v = v.astype(F32)
    r = lax.rsqrt(jnp.mean(v * v, axis=-1, keepdims=True) + EPS)
    return (v * r * w.astype(F32)).astype(BF)


def _ffn(u, w1, w3, w2):
    g = jnp.dot(u, w1, preferred_element_type=F32)
    v = jnp.dot(u, w3, preferred_element_type=F32)
    z = (jax.nn.silu(g) * v).astype(BF)
    return jnp.dot(z, w2, preferred_element_type=F32).astype(BF)


def _experts(xin, w1, w3, w2):
    g = jnp.einsum('erd,edf->erf', xin, w1, preferred_element_type=F32)
    v = jnp.einsum('erd,edf->erf', xin, w3, preferred_element_type=F32)
    z = (jax.nn.silu(g) * v).astype(BF)
    return jnp.einsum('erf,efd->erd', z, w2, preferred_element_type=F32).astype(BF)


def _attn(x, kk, vv, lens, ln1, wq, wo):
    b, l, kvh, dh = kk.shape
    hq = wq.shape[1] // dh
    a = _rms(x, ln1)
    q = jnp.dot(a, wq, preferred_element_type=F32).astype(BF).reshape(b, kvh, hq // kvh, dh)
    s = jnp.einsum('bkgd,blkd->bkgl', q, kk, preferred_element_type=F32) * dh ** -0.5
    valid = jnp.arange(l)[None, :] < lens[:, None]
    s = jnp.where(valid[:, None, None, :], s, -jnp.inf)
    p = jax.nn.softmax(s, axis=-1).astype(BF)
    o = jnp.einsum('bkgl,blkd->bkgd', p, vv, preferred_element_type=F32).astype(BF)
    attn = jnp.dot(o.reshape(b, hq * dh), wo, preferred_element_type=F32)
    return (x.astype(F32) + attn).astype(BF)


def _ranks(topk, n_exp):
    chosen = (topk[..., None] == jnp.arange(n_exp)).any(axis=-2).astype(jnp.int32)
    before = jnp.cumsum(chosen, axis=-2) - chosen
    return jnp.take_along_axis(before, topk, axis=-1)


def solution(mesh):
    ey, ex = mesh.shape['ey'], mesh.shape['ex']
    ndev = ey * ex
    rows = P(('ey', 'ex'))
    rep = P()

    def local(x, kv_k, kv_v, lens, topk_idx, gates, ln1, ln2, wq, wo, ws1, ws3, ws2, w1, w3, w2):
        b, d = x.shape
        k = topk_idx.shape[1]
        edev = w1.shape[0]
        n_exp = edev * ndev
        cap = max(4, (2 * b * k + n_exp - 1) // n_exp)
        nslotv = ex * edev * ey * cap
        iy = lax.axis_index('ey')

        h = _attn(x, kv_k, kv_v, lens, ln1, wq, wo)
        u = _rms(h, ln2)

        u_g = lax.all_gather(u, 'ey')
        t_g = lax.all_gather(topk_idx, 'ey')
        g_g = lax.all_gather(gates, 'ey')

        rank = _ranks(t_g, n_exp)
        mine = (t_g // (edev * ex) == iy) & (rank < cap)
        src = jnp.arange(ey, dtype=jnp.int32)[:, None, None]
        dest = ((t_g // edev) % ex) * edev + t_g % edev
        pos = jnp.where(mine, (dest * ey + src) * cap + rank, nslotv).reshape(-1)
        tok = jnp.broadcast_to(jnp.arange(ey * b, dtype=jnp.int32).reshape(ey, b, 1), t_g.shape).reshape(-1)
        slot_tok = jnp.full((nslotv,), ey * b, jnp.int32).at[pos].set(tok, mode='drop')
        slot_gate = jnp.zeros((nslotv,), F32).at[pos].set(g_g.reshape(-1), mode='drop')
        u_pad = jnp.concatenate([u_g.reshape(ey * b, d), jnp.zeros((1, d), BF)], axis=0)

        send = u_pad[slot_tok].reshape(ex, edev, ey * cap, d)
        recv = lax.all_to_all(send, 'ex', 0, 0)
        xin = recv.transpose(1, 0, 2, 3).reshape(edev, ex * ey * cap, d)
        out = _experts(xin, w1, w3, w2)
        back = out.reshape(edev, ex, ey * cap, d).transpose(1, 0, 2, 3)
        ret = lax.all_to_all(back, 'ex', 0, 0).reshape(nslotv, d)

        partial = jnp.zeros((ey * b + 1, d), F32).at[slot_tok].add(slot_gate[:, None] * ret.astype(F32))
        routed = lax.psum_scatter(partial[: ey * b].reshape(ey, b, d), 'ey', scatter_dimension=0)
        y = h.astype(F32) + _ffn(u, ws1, ws3, ws2).astype(F32) + routed
        return y.astype(BF)

    return jax.shard_map(
        local, mesh=mesh,
        in_specs=(rows, rows, rows, rows, rows, rows, rep, rep, rep, rep, rep, rep, rep, rows, rows, rows),
        out_specs=rows, check_vma=False)
```

profile of v0, /device:TPU:0, one launch (start us, length us, event | category | flops | bytes accessed | tf_op | source)
XLA Modules:
  0.0 251.8 jit_solution(7787265754273803269)
XLA Ops:
  6.5 0.7 convert_element_type.62
  7.2 1.1 fusion.28
  8.4 5.1 %fusion.25 = bf16[8,8,16,128]{3,1,2,0:T(8,128)(2,1)S(1)} fusion(bf16[2048,2048]{1,0:T(8,128)(2,1)} %param.24, bf16[64,2048]{1,0:T(8,128)(2,1)} %param.16, f32[2048]{0:T(1024)S(1)} %convert_element_type.62, f32[64]{0:T(128)S(1)} %add_rsqrt_fusion.1), kind=kOutput, calls=%fused_computation.32 | convolution fusion | flops 537526272 | bytes 8921344 | tf_op jit(solution)/shard_map/dot_general | solution.py:35
  13.6 3.6 %fusion.59 = (f32[64,16]{1,0:T(8,128)S(1)}, f32[64,16,256]{2,1,0:T(8,128)S(1)}) fusion(bf16[64,16,128]{2,1,0:T(8,128)(2,1)S(1)} %bitcast.65, bf16[64,256,1,128]{3,1,2,0:T(8,128)(2,1)} %param.17, pred[64,256]{1,0:T(8,128)(4,1)S(1)} %iota_compare_fusion.1), kind=kOutput, calls=%fused_computation.93 | convolution fusion | flops 68157696 | bytes 5525504 | tf_op jit(solution)/shard_map/sub | solution.py:39
  17.2 3.0 %fusion.22 = bf16[64,16,128]{2,1,0:T(8,128)(2,1)S(1)} fusion(bf16[64,256,1,128]{3,1,2,0:T(8,128)(2,1)} %param.18, f32[64,16,256]{2,1,0:T(8,128)S(1)} %get-tuple-element.6, f32[64,16]{1,0:T(8,128)S(1)} %get-tuple-element.5), kind=kOutput, calls=%fused_computation.31 | convolution fusion | flops 67764224 | bytes 5509120 | tf_op jit(solution)/shard_map/bkgl,blkd->bkgd/dot_general | solution.py:40
  20.2 5.1 %multiply_reduce_fusion = (f32[64]{0:T(128)S(1)}, f32[64,2048]{1,0:T(8,128)S(1)}) fusion(bf16[2048,2048]{1,0:T(8,128)(2,1)} %param.25, bf16[8,8,16,128]{3,2,1,0:T(8,128)(2,1)S(1)} %bitcast.66, bf16[64,2048]{1,0:T(8,128)(2,1)S(1)} %copy-done.3), kind=kOutput, calls=%fused_computation.43 | convolution fusion | flops 537657280 | bytes 9437440 | tf_op jit(solution)/shard_map/dot_general | solution.py:41
  25.3 0.8 copy-done
  26.1 0.8 multiply_convert_fusion.1
  26.9 14.8 %all-gather.3 = s32[4,64,6]{1,2,0:T(8,128)S(1)} all-gather(s32[1,64,6]{1,2,0:T(8,128)S(1)} %bitcast.67), channel_id=2, replica_groups=mesh['ey'=4,'ex'=8] {'ey'}, dimensions={0}, use_global_device_ids=true | all-gather | bytes 7680 | tf_op jit(solution)/shard_map/all_gather | solution.py:70
  41.7 0.3 fusion.27
  42.3 0.1 reduce_window_sum.11
  42.4 12.6 %gather_fusion.1 = s32[1536]{0:T(1024)S(1)} fusion(s32[4,64,64]{2,1,0:T(8,128)S(1)} %convert_subtract_fusion, s32[1536]{0:T(1024)S(1)} %reshape.181), kind=kCustom, calls=%fused_computation.1 | custom fusion | bytes 30720 | tf_op jit(solution)/shard_map/jit(take_along_axis)/gather | solution.py:48
  55.5 0.1 reshape.161
  55.8 0.1 reshape.191
  56.0 6.2 %scatter_custom_fusion = s32[768]{0:T(1024)S(1)} fusion(s32[1536]{0:T(1024)S(1)} %fusion.53, s32[1536]{0:T(1024)S(1)} %reshape.191, s32[]{:T(128)} %constant.91.clone.1), kind=kCustom, calls=%fused_computation.88 | custom fusion | bytes 3076 | tf_op jit(solution)/shard_map/scatter | solution.py:79
  62.2 1.3 concatenate.3
  63.5 4.3 %gather_fusion = bf16[768,2048]{1,0:T(8,128)(2,1)} fusion(bf16[257,2048]{1,0:T(8,128)(2,1)S(1)} %concatenate.3, s32[1024]{0:T(1024)S(1)} %pad_clamp_fusion), kind=kCustom, calls=%fused_computation | custom fusion | bytes 6294528 | tf_op jit(solution)/shard_map/gather | solution.py:83
  67.8 41.3 %all_to_all.10 = bf16[8,2,48,2048]{3,2,1,0:T(8,128)(2,1)S(1)} all-to-all(bf16[8,2,48,2048]{3,2,1,0:T(8,128)(2,1)} %bitcast.60), channel_id=1, replica_groups=mesh['ey'=4,'ex'=8] {'ex'}, dimensions={0} | all-to-all | bytes 6291456 | tf_op jit(solution)/shard_map/all_to_all | solution.py:84
  109.1 0.4 copy.55
  109.6 10.1 %fusion.63 = f32[2,384,1408]{2,1,0:T(8,128)} fusion(bf16[2,384,2048]{2,1,0:T(8,128)(2,1)S(1)} %bitcast.62, bf16[2,2048,1408]{2,1,0:T(8,128)(2,1)} %param.29), kind=kOutput, calls=%fused_computation.95 | convolution fusion | flops 4429185024 | bytes 19005440 | tf_op jit(solution)/shard_map/erd,edf->erf/dot_general | solution.py:25
  119.7 7.2 %multiply_convert_fusion = bf16[2,384,1408]{2,1,0:T(8,128)(2,1)S(1)} fusion(f32[2,384,1408]{2,1,0:T(8,128)} %fusion.63, bf16[2,384,2048]{2,1,0:T(8,128)(2,1)S(1)} %bitcast.63, bf16[2,2048,1408]{2,1,0:T(8,128)(2,1)S(1)} %bitcast.70), kind=kOutput, calls=%fused_computation.8 | convolution fusion | flops 4435673088 | bytes 21168128 | tf_op jit(solution)/shard_map/erd,edf->erf/dot_general | solution.py:26
  127.0 5.2 %convolution_convert_fusion = bf16[2,384,2048]{2,1,0:T(8,128)(2,1)S(1)} fusion(bf16[2,384,1408]{2,1,0:T(8,128)(2,1)S(1)} %multiply_convert_fusion, bf16[2,1408,2048]{2,1,0:T(8,128)(2,1)S(1)} %bitcast.72), kind=kOutput, calls=%fused_computation.13 | convolution fusion | flops 4430757888 | bytes 16842752 | tf_op jit(solution)/shard_map/erf,efd->erd/dot_general | solution.py:28
  132.3 1.9 copy.68
  134.2 3.8 %all-to-all-start.1 = ((bf16[8,2,48,2048]{3,2,1,0:T(8,128)(2,1)}), bf16[8,2,48,2048]{3,2,1,0:T(8,128)(2,1)S(1)}, u32[]{:S(2)}, u32[]{:S(2)}) async-start(bf16[8,2,48,2048]{3,2,1,0:T(8,128)(2,1)} %bitcast.58), calls=%async_computation.1 | async-start | bytes 6291456 | tf_op jit(solution)/shard_map/all_to_all | solution.py:88
  138.0 13.0 %all-gather.4 = f32[4,64,6]{1,2,0:T(8,128)S(1)} all-gather(f32[1,64,6]{1,2,0:T(8,128)S(1)} %bitcast.68), channel_id=3, replica_groups=mesh['ey'=4,'ex'=8] {'ey'}, dimensions={0}, use_global_device_ids=true | all-gather | bytes 7680 | tf_op jit(solution)/shard_map/all_gather | solution.py:71
  151.3 6.4 %scatter_custom_fusion.1 = f32[768]{0:T(1024)S(1)} fusion(s32[1536]{0:T(1024)S(1)} %fusion.53, f32[1536]{0:T(1024)S(1)} %reshape.199, f32[]{:T(128)} %constant.85.clone.1), kind=kCustom, calls=%fused_computation.85 | custom fusion | bytes 3076 | tf_op jit(solution)/shard_map/scatter | solution.py:80
  157.7 18.0 %all-to-all-done.1 = bf16[8,2,48,2048]{3,2,1,0:T(8,128)(2,1)S(1)} async-done(((bf16[8,2,48,2048]{3,2,1,0:T(8,128)(2,1)}), bf16[8,2,48,2048]{3,2,1,0:T(8,128)(2,1)S(1)}, u32[]{:S(2)}, u32[]{:S(2)}) %all-to-all-start.1) | async-done | bytes 3145760 | tf_op jit(solution)/shard_map/all_to_all | solution.py:88
  175.7 15.4 %scatter_custom_fusion.2 = f32[257,2048]{1,0:T(8,128)} fusion(s32[768]{0:T(1024)S(1)} %compare_select_fusion.1, bf16[768,2048]{1,0:T(8,128)(2,1)S(1)} %bitcast.57, f32[768]{0:T(1024)S(1)} %scatter_custom_fusion.1, f32[]{:T(128)} %constant.85.clone.1), kind=kCustom, calls=%fused_computation.7 | custom fusion | flops 4718592 | bytes 5255172 | tf_op jit(solution)/shard_map/scatter-add | solution.py:90
  191.1 3.2 %slice.9 = f32[256,2048]{1,0:T(8,128)} slice(f32[257,2048]{1,0:T(8,128)} %scatter_custom_fusion.2), slice={[0:256], [0:2048]} | slice | bytes 4194304 | tf_op jit(solution)/shard_map/slice | solution.py:91
  194.3 3.8 %fusion.62 = f32[64,1408]{1,0:T(8,128)S(1)} fusion(bf16[64,2048]{1,0:T(8,128)(2,1)S(1)} %copy-done.2, bf16[2048,1408]{1,0:T(8,128)(2,1)} %param.26), kind=kOutput, calls=%fused_computation.94 | convolution fusion | flops 369098752 | bytes 6389760 | tf_op jit(solution)/shard_map/dot_general | solution.py:18
  198.1 39.7 %reduce-scatter.2.cloned.1.call-done = f32[1,64,2048]{2,1,0:T(8,128)} async-done(((f32[4,64,2048]{2,1,0:T(8,128)}), f32[1,64,2048]{2,1,0:T(8,128)}) %reduce-scatter.2.cloned.1.call-update) | async-done | bytes 524304 | tf_op jit(solution)/shard_map/reduce_scatter | solution.py:91
  237.8 7.2 %fusion.13 = bf16[64,2048]{1,0:T(8,128)(2,1)} fusion(f32[64,2048]{1,0:T(8,128)S(1)} %copy-done.1, bf16[1408,2048]{1,0:T(8,128)(2,1)} %param.28, bf16[64,2048]{1,0:T(8,128)(2,1)S(1)} %copy-done.2, bf16[2048,1408]{1,0:T(8,128)(2,1)} %param.27, f32[1,64,2048]{2,1,0:T(8,128)} %reduce-scatter.2.cloned.1.call-done, f32[64,1408]{1,0:T(8,128)S(1)} %fusion.62), kind=kOutput, calls=%fused_computation.25 | convolution fusion | flops 739393536 | bytes 13467648 | tf_op jit(solution)/shard_map/dot_general | solution.py:21
  (55 shorter events, 1.4 us)
Async XLA Ops:
  6.5 55.7 %all-gather.7.cloned.1.call-start = ((), (), s32[]{:S(2)}) async-start(), calls=%async_computation.4 | async-start | bytes 1310720 | tf_op jit(solution)/shard_map/all_gather | solution.py:69
  8.3 5.2 %copy-start.7 = (s32[64]{0:T(128)S(1)}, s32[64]{0:T(128)}, u32[]{:S(2)}) copy-start(s32[64]{0:T(128)} %param.19) | copy-start | bytes 772
  17.2 3.0 %copy-start.3 = (bf16[64,2048]{1,0:T(8,128)(2,1)S(1)}, bf16[64,2048]{1,0:T(8,128)(2,1)}, u32[]{:S(2)}) copy-start(bf16[64,2048]{1,0:T(8,128)(2,1)} %param.16) | copy-start | bytes 786436
  20.1 5.1 %copy-start.4 = (bf16[2048]{0:T(1024)(128)(2,1)S(1)}, bf16[2048]{0:T(1024)(128)(2,1)}, u32[]{:S(2)}) copy-start(bf16[2048]{0:T(1024)(128)(2,1)} %param.23) | copy-start | bytes 12292
  20.2 6.8 %copy-start.5 = (s32[64,6]{0,1:T(8,128)S(1)}, s32[64,6]{0,1:T(8,128)}, u32[]{:S(2)}) copy-start(s32[64,6]{0,1:T(8,128)} %param.20) | copy-start | bytes 4612
  25.3 0.8 copy-start
  109.1 10.6 %slice-start = ((s8[11534336]{0:T(1024)(128)(4,1)}), s8[4194304]{0:T(1024)(128)(4,1)S(1)}, s32[]{:S(2)}) async-start(s8[11534336]{0:T(1024)(128)(4,1)} %bitcast.69), calls=%async_computation.5 | async-start | bytes 8388608
  109.5 10.2 %slice-start.1 = ((s8[11534336]{0:T(1024)(128)(4,1)}), s8[4194304]{0:T(1024)(128)(4,1)S(1)}, s32[]{:S(2)}) async-start(s8[11534336]{0:T(1024)(128)(4,1)} %bitcast.69), calls=%async_computation.6 | async-start | bytes 8388608
  109.5 10.2 %slice-start.2 = ((s8[11534336]{0:T(1024)(128)(4,1)}), s8[3145728]{0:T(1024)(128)(4,1)S(1)}, s32[]{:S(2)}) async-start(s8[11534336]{0:T(1024)(128)(4,1)} %bitcast.69), calls=%async_computation.7 | async-start | bytes 6291456
  109.5 17.4 %slice-start.3 = ((s8[11534336]{0:T(1024)(128)(4,1)}), s8[4194304]{0:T(1024)(128)(4,1)S(1)}, s32[]{:S(2)}) async-start(s8[11534336]{0:T(1024)(128)(4,1)} %bitcast.71), calls=%async_computation.8 | async-start | bytes 8388608
  119.7 7.3 %slice-start.4 = ((s8[11534336]{0:T(1024)(128)(4,1)}), s8[4194304]{0:T(1024)(128)(4,1)S(1)}, s32[]{:S(2)}) async-start(s8[11534336]{0:T(1024)(128)(4,1)} %bitcast.71), calls=%async_computation.9 | async-start | bytes 8388608
  119.7 7.3 %slice-start.5 = ((s8[11534336]{0:T(1024)(128)(4,1)}), s8[3145728]{0:T(1024)(128)(4,1)S(1)}, s32[]{:S(2)}) async-start(s8[11534336]{0:T(1024)(128)(4,1)} %bitcast.71), calls=%async_computation.10 | async-start | bytes 6291456
  134.2 3.8 %copy-start.6 = (f32[64,6]{0,1:T(8,128)S(1)}, f32[64,6]{0,1:T(8,128)}, u32[]{:S(2)}) copy-start(f32[64,6]{0,1:T(8,128)} %param.21) | copy-start | bytes 4612
  134.2 41.6 %all-to-all-start.1 = ((bf16[8,2,48,2048]{3,2,1,0:T(8,128)(2,1)}), bf16[8,2,48,2048]{3,2,1,0:T(8,128)(2,1)S(1)}, u32[]{:S(2)}, u32[]{:S(2)}) async-start(bf16[8,2,48,2048]{3,2,1,0:T(8,128)(2,1)} %bitcast.58), calls=%async_computation.1 | async-start | bytes 6291456 | tf_op jit(solution)/shard_map/all_to_all | solution.py:88
  137.9 99.8 %reduce-scatter.2.cloned.1.call-start = ((), (), s32[]{:S(2)}) async-start(), calls=%async_computation.3 | async-start | bytes 2621440 | tf_op jit(solution)/shard_map/reduce_scatter | solution.py:91
  191.1 3.2 %copy-start.2 = (bf16[64,2048]{1,0:T(8,128)(2,1)S(1)}, bf16[64,2048]{1,0:T(8,128)(2,1)}, u32[]{:S(2)}) copy-start(bf16[64,2048]{1,0:T(8,128)(2,1)} %multiply_convert_fusion.1) | copy-start | bytes 786436
  194.3 43.5 %copy-start.1 = (f32[64,2048]{1,0:T(8,128)S(1)}, f32[64,2048]{1,0:T(8,128)}, u32[]{:S(2)}) copy-start(f32[64,2048]{1,0:T(8,128)} %copy-done) | copy-start | bytes 1572868
Sparse Core Ops, SparseCore 0:
  27.0 30.7 all-gather.6
  194.4 43.3 reduce-scatter.1
where the time goes:
time: 252 us
  blocking collectives  69.2 us (27%)
  waiting for transfers between devices  57.8 us (23%)
  matrix products  50.2 us (20%)
  local copies, waits for them, and re-layouts  38.3 us (15%)
  other arithmetic  18.6 us (7%)
  between operations  13.8 us (5%)
  starting transfers between devices  3.82 us (2%)
    all_to_all x1, blocking collectives, local(): recv = lax.all_to_all(send, 'ex', 0, 0)  41.3 us
    reduce_scatter x1, waiting for transfers between devices, local(): lax.psum_scatter(partial[:ey * b].reshape(ey, b, d), 'ey', scatter_dimens...  39.7 us
    all_to_all x1, waiting for transfers between devices, local(): ret = lax.all_to_all(back, 'ex', 0, 0).reshape(nslotv, d)  18 us
    scatter-add x1, other arithmetic, local(): jnp.zeros((ey * b + 1, d), F32).at[slot_tok]  15.4 us
    all_gather x1, blocking collectives, local(): t_g = lax.all_gather(topk_idx, 'ey')  14.8 us
    gather x5, local copies, waits for them, and re-layouts, _ranks(): return jnp.take_along_axis(before, topk, axis=-1)  13.1 us
    all_gather x1, blocking collectives, local(): g_g = lax.all_gather(gates, 'ey')  13 us
    dot_general x1, matrix products, _experts(): g = jnp.einsum('erd,edf->erf', xin, w1, preferred_element_type=F32)  10.1 us
  transfers between devices with their start and end apart: 3, of which 2 were waited for; matrix products, arithmetic and copies ran while one was open for 12% of the time, Pallas kernels for 0%

commit v1 on v0

v1 whole, which is shorter than its diff:
```python
import functools

import jax
import jax.numpy as jnp
from jax import lax
from jax.experimental import pallas as pl
from jax.experimental.pallas import tpu as pltpu
from jax.sharding import PartitionSpec as P

EPS = 1e-6
BF = jnp.bfloat16
F32 = jnp.float32
MESH = pl.DeviceIdType.MESH
META = 128
VMEM = pltpu.VMEM
ANY = pl.ANY


def _dot(a, b):
    return jnp.dot(a, b, preferred_element_type=F32)


def _dot_nt(a, b):
    return lax.dot_general(a, b, (((1,), (1,)), ((), ())), preferred_element_type=F32)


def _rms(v, w):
    v = v.astype(F32)
    r = lax.rsqrt(jnp.mean(v * v, axis=-1, keepdims=True) + EPS)
    return (v * r * w.astype(F32)).astype(BF)


def _split3(v):
    p1 = v.astype(BF)
    v = v - p1.astype(F32)
    p2 = v.astype(BF)
    p3 = (v - p2.astype(F32)).astype(BF)
    return p1, p2, p3


def _attn_kernel(nrow, n_exp, C, cap, lens, x, topk, gates, ln1, ln2, kk, vv, wq, wo,
                 h_out, u_out, xc_out, back_out,
                 wqv, wov, kv, vvv, qs, os, sw, so, sk, sv):
    b, d = x.shape
    l, dh = kk.shape[1], kk.shape[2]
    nh = wq.shape[1] // dh
    nw = sw.shape[0]
    wc = d // nw
    nk = sk.shape[0]
    tk = b // nk
    nt = topk.shape[0]

    def cq(i):
        return pltpu.make_async_copy(wq.at[:, pl.ds(i * wc, wc)], wqv.at[i], sw.at[i])

    def co(i):
        return pltpu.make_async_copy(wo.at[:, pl.ds(i * wc, wc)], wov.at[i], so.at[i])

    def ck(i):
        return pltpu.make_async_copy(kk.at[pl.ds(i * tk, tk)], kv.at[pl.ds(i * tk, tk)], sk.at[i])

    def cv(i):
        return pltpu.make_async_copy(vv.at[pl.ds(i * tk, tk)], vvv.at[pl.ds(i * tk, tk)], sv.at[i])

    for i in range(nw):
        cq(i).start()
    for i in range(nk):
        ck(i).start()
        cv(i).start()
    for i in range(nw):
        co(i).start()

    eio = lax.broadcasted_iota(jnp.int32, (n_exp, b), 0)
    ch = jnp.zeros((n_exp, b), F32)
    gt = jnp.zeros((n_exp, b), F32)
    for j in range(nt):
        hit = eio == topk[j:j + 1, :]
        ch = jnp.where(hit, 1.0, ch)
        gt = jnp.where(hit, gates[j:j + 1, :], gt)
    upper = (lax.broadcasted_iota(jnp.int32, (b, b), 0) < lax.broadcasted_iota(jnp.int32, (b, b), 1))
    upper = jnp.where(upper, 1.0, 0.0).astype(BF)
    rank = _dot(ch.astype(BF), upper)
    kept = (ch > 0) & (rank < cap)
    kp1 = jnp.where(kept, rank + 1.0, 0.0)
    g1, g2, g3 = _split3(jnp.where(kept, gt, 0.0))
    er = n_exp // nrow
    sels, metas = [], []
    cio = lax.broadcasted_iota(jnp.int32, (C, b), 0).astype(F32)
    for r in range(nrow):
        sl = slice(r * er, (r + 1) * er)
        need = jnp.max(jnp.where(kept[sl], 1.0, 0.0), axis=0, keepdims=True)
        need8 = jnp.broadcast_to(need, (8, b))
        cpos = _dot(need8.astype(BF), upper)[0:1]
        sel = jnp.where((cio == cpos) & (need > 0), 1.0, 0.0).astype(BF)
        sels.append(sel)
        m = jnp.concatenate([kp1[sl], g1[sl].astype(F32), g2[sl].astype(F32), g3[sl].astype(F32),
                             jnp.zeros((META - 4 * er, b), F32)], axis=0).astype(BF)
        metas.append(_dot_nt(sel, m).astype(BF))
    eye = (lax.broadcasted_iota(jnp.int32, (b, b), 0) == lax.broadcasted_iota(jnp.int32, (b, b), 1))
    eye = jnp.where(eye, 1.0, 0.0).astype(BF)
    selall = jnp.concatenate(sels, axis=0)
    back_out[...] = _dot_nt(eye, selall).astype(BF)

    a = _rms(x[...], ln1[...])
    hc = wc // dh
    for i in range(nw):
        cq(i).wait()
        q = _dot(a, wqv[i]).astype(BF).astype(F32)
        for j in range(hc):
            qs[:, i * hc + j, :] = q[:, j * dh:(j + 1) * dh]

    scale = dh ** -0.5
    lio = lax.broadcasted_iota(jnp.int32, (nh, l), 1)
    un = 8

    def group(g, _):
        for i in range(nk):
            @pl.when(g * un == i * tk)
            def _():
                ck(i).wait()
                cv(i).wait()
        ts = [g * un + j for j in range(un)]
        ss = [_dot_nt(qs[t].astype(BF), kv[t]) for t in ts]
        ps = []
        for t, s in zip(ts, ss):
            s = jnp.where(lio < lens[t], s * scale, -jnp.inf)
            p = jnp.exp(s - jnp.max(s, axis=-1, keepdims=True))
            ps.append((p * (1.0 / jnp.sum(p, axis=-1, keepdims=True))).astype(BF))
        for t, p in zip(ts, ps):
            os[t] = _dot(p, vvv[t])
        return 0

    lax.fori_loop(0, b // un, group, 0)
    o = jnp.concatenate([os[:, j, :].astype(BF) for j in range(nh)], axis=1)
    hs = []
    for i in range(nw):
        co(i).wait()
        hs.append((x[:, i * wc:(i + 1) * wc].astype(F32) + _dot(o, wov[i])).astype(BF))
    h = jnp.concatenate(hs, axis=1)
    h_out[...] = h
    u = _rms(h, ln2[...])
    u_out[...] = u
    xall = _dot(selall, u).astype(BF)
    for r in range(nrow):
        xc_out[r, :, :d] = xall[r * C:(r + 1) * C]
        xc_out[r, :, d:] = metas[r]


def _attention(x, kk, vv, lens, topk_t, gates_t, ln1, ln2, wq, wo, nrow, n_exp, C, cap):
    b, d = x.shape
    _, l, _, dh = kk.shape
    kk, vv = kk.reshape(b, l, dh), vv.reshape(b, l, dh)
    nw, nk = 4, 4
    nh = wq.shape[1] // dh
    vm = pl.BlockSpec(memory_space=VMEM)
    an = pl.BlockSpec(memory_space=ANY)
    return pl.pallas_call(
        functools.partial(_attn_kernel, nrow, n_exp, C, cap),
        out_shape=[jax.ShapeDtypeStruct((b, d), BF), jax.ShapeDtypeStruct((b, d), BF),
                   jax.ShapeDtypeStruct((nrow, C, d + META), BF), jax.ShapeDtypeStruct((b, nrow * C), BF)],
        in_specs=[pl.BlockSpec(memory_space=pltpu.SMEM)] + [vm] * 5 + [an] * 4,
        out_specs=[vm] * 4,
        scratch_shapes=[
            pltpu.VMEM((nw, d, d // nw), BF), pltpu.VMEM((nw, d, d // nw), BF),
            pltpu.VMEM((b, l, dh), BF), pltpu.VMEM((b, l, dh), BF),
            pltpu.VMEM((b, nh, dh), F32), pltpu.VMEM((b, nh, dh), F32),
            pltpu.SemaphoreType.DMA((nw,)), pltpu.SemaphoreType.DMA((nw,)),
            pltpu.SemaphoreType.DMA((nk,)), pltpu.SemaphoreType.DMA((nk,)),
        ],
        name='attention',
        compiler_params=pltpu.CompilerParams(vmem_limit_bytes=56 * 2 ** 20),
    )(lens, x, topk_t, gates_t, ln1.reshape(1, d), ln2.reshape(1, d), kk, vv, wq, wo)


def _xor(a, b, bits):
    r = 0
    for i in range(bits):
        m = 2 ** i
        p, q = (a // m) % 2, (b // m) % 2
        r = r + m * ((p + q) % 2)
    return r


def _moe_kernel(ney, nex, C, cap, nj, fb,
                xc, h, u, back, ws1, ws3, ws2, w1, w3, w2, y,
                T, w1v, w3v, w2v, sa, sb, xin, act, O, R, PS, Q, G, acc, shr,
                s_loc, zs, zr, xs, xr, ys, yr, ds_, dr, ps, pr, s_w, s_w2, s_sa, s_sb, r1s, r1r, r2s, r2r):
    d = u.shape[1]
    edev, _, ff = w1.shape
    erow = edev * nex
    z = lax.axis_index('ey')
    e = lax.axis_index('ex')
    core, x, yy = e % 2, (e // 2) % 2, e // 4
    xn = yy * 4 + (1 - x) * 2 + core
    yn = (1 - yy) * 4 + x * 2 + core
    dg = (1 - yy) * 4 + (1 - x) * 2 + core
    pt = yy * 4 + x * 2 + (1 - core)
    H = C // 2

    def zx(i):
        return _xor(z, i, 2)

    def rcopy(src, dst, ss, rs, dev):
        return pltpu.make_async_remote_copy(src_ref=src, dst_ref=dst, send_sem=ss, recv_sem=rs,
                                            device_id=dev, device_id_type=MESH)

    ka = sa.shape[2]
    kb = sb.shape[1]
    na, nb = d // ka, ff // kb

    def c_a(i, slot):
        return [pltpu.make_async_copy(w.at[pl.ds(i * ka, ka)], sa.at[slot, m], s_sa.at[slot, m])
                for m, w in enumerate((ws1, ws3))]

    def c_b(i, slot):
        return pltpu.make_async_copy(ws2.at[pl.ds(i * kb, kb)], sb.at[slot], s_sb.at[slot])

    def c_w(m, k):
        src, dst = ((w1, w1v), (w3, w3v))[m]
        return pltpu.make_async_copy(src.at[k], dst.at[k], s_w.at[m, k])

    jc = d // nj

    def c_w2(j, slot):
        return pltpu.make_async_copy(w2.at[:, :, pl.ds(pl.multiple_of(j * jc, jc), jc)], w2v.at[slot], s_w2.at[slot])

    loc = pltpu.make_async_copy(xc.at[z], T.at[e, z], s_loc)
    loc.start()
    for i in range(2):
        for c in c_a(i, i):
            c.start()
    c_b(0, 0).start()
    c_b(1, 1).start()

    bar = pltpu.get_barrier_semaphore()
    peers = [(zx(i), e) for i in range(1, ney)] + [(z, _xor(e, q, 3)) for q in range(1, nex)]
    for dev in peers:
        pl.semaphore_signal(bar, inc=1, device_id=dev, device_id_type=MESH)
    pl.semaphore_wait(bar, len(peers))

    zc = [None] + [rcopy(xc.at[zx(i)], T.at[e, z], zs.at[i], zr.at[i], (zx(i), e)) for i in range(1, ney)]
    zw = [None] + [rcopy(xc.at[z], T.at[e, zx(i)], zs.at[i], zr.at[i], (zx(i), e)) for i in range(1, ney)]
    for i in range(1, ney):
        zc[i].start()
    for m in range(2):
        for k in range(edev):
            c_w(m, k).start()
    c_w2(0, 0).start()
    c_w2(1, 1).start()

    def half(c, s, hf):
        return T.at[c, s, pl.ds(hf * H, H)]

    def fwd(c, s, hf, ssem, rsem, dst):
        return rcopy(half(c, s, hf), half(c, s, hf), ssem, rsem, (z, dst))

    def to_x(i, hf):
        return fwd(e, zx(i), hf, xs.at[i, hf], xr.at[i, hf], xn)

    def to_y(i, hf):
        return fwd(e, zx(i), hf, ys.at[i, hf], yr.at[i, hf], yn)

    def to_d(i, hf):
        return fwd((xn, yn)[hf], zx(i), hf, ds_.at[i, hf], dr.at[i, hf], (yn, xn)[hf])

    def to_p(i, k):
        blk = T.at[(e, xn, yn, dg)[k], zx(i)]
        return rcopy(blk, blk, ps.at[i, k], pr.at[i, k], (z, pt))

    def stage1(i):
        if i == 0:
            loc.wait()
        else:
            zw[i].wait_recv()
        for hf in (0, 1):
            to_x(i, hf).start()
            to_y(i, 1 - hf).start()
        to_p(i, 0).start()

    def stage2(i):
        to_x(i, 0).wait_recv()
        to_d(i, 0).start()
        to_y(i, 1).wait_recv()
        to_d(i, 1).start()
        to_x(i, 1).wait_recv()
        to_p(i, 1).start()
        to_y(i, 0).wait_recv()
        to_p(i, 2).start()

    def stage3(i):
        to_d(i, 0).wait_recv()
        to_d(i, 1).wait_recv()
        to_p(i, 3).start()

    def shared_a():
        acc[...] = jnp.zeros_like(acc)

        def body(i, _):
            slot = i % 2
            for c in c_a(i, slot):
                c.wait()
            uc = u[:, pl.ds(pl.multiple_of(i * ka, ka), ka)]
            acc[0] += _dot(uc, sa[slot, 0])
            acc[1] += _dot(uc, sa[slot, 1])

            @pl.when(i + 2 < na)
            def _():
                for c in c_a(i + 2, slot):
                    c.start()
            return 0
        lax.fori_loop(0, na, body, 0)

    def shared_b():
        shr[...] = jnp.zeros_like(shr)
        zz = (jax.nn.silu(acc[0]) * acc[1]).astype(BF)
        for i in range(nb):
            slot = i % 2
            c_b(i, slot).wait()
            shr[...] += _dot(zz[:, i * kb:(i + 1) * kb], sb[slot])
            if i + 2 < nb:
                c_b(i + 2, slot).start()
        shr[...] = shr[...].astype(BF).astype(F32)

    def combine_matrix():
        M = T[e, :, :, d:].reshape(ney * C, META)
        n = erow * ney * cap
        ln = lax.broadcasted_iota(jnp.int32, (META, n), 1)
        er = lax.broadcasted_iota(jnp.int32, (META, n), 0)
        sp = ln // (ney * cap)
        ex = [jnp.where(er == sp + m * erow, 1.0, 0.0).astype(BF) for m in range(4)]
        k1 = _dot(M, ex[0])
        srow = lax.broadcasted_iota(jnp.int32, (ney * C, n), 0) // C
        pos = lax.broadcasted_iota(jnp.int32, (ney * C, n), 1) % (ney * cap)
        hit = (k1 > 0) & ((k1 + (srow * cap - 1).astype(F32)) == pos.astype(F32))
        for m in range(3):
            G[m] = jnp.where(hit, _dot(M, ex[m + 1]), 0.0).astype(BF)

    def gather(c, _):
        M = T[c, :, :, d:].reshape(ney * C, META)
        sel = (lax.broadcasted_iota(jnp.int32, (16, META), 1)
               == lax.broadcasted_iota(jnp.int32, (16, META), 0) + edev * e)
        sel = jnp.where(sel, 1.0, 0.0).astype(BF)
        V = _dot_nt(sel, M)
        rows = ney * cap
        s = lax.broadcasted_iota(jnp.int32, (1, ney * C), 1) // C
        pos = lax.broadcasted_iota(jnp.int32, (rows, ney * C), 0).astype(F32)
        X = T[c, :, :, :d].reshape(ney * C, d)
        for k in range(edev):
            v = V[k:k + 1]
            tgt = jnp.where(v > 0, v + (s * cap - 1).astype(F32), -1.0)
            xin[k, c] = _dot(jnp.where(pos == tgt, 1.0, 0.0).astype(BF), X).astype(BF)
        return 0

    stage1(0)
    shared_a()
    stage1(1)
    stage2(0)
    shared_b()
    stage1(2)
    stage2(1)
    stage3(0)
    stage1(3)
    combine_matrix()
    stage2(2)
    stage3(1)
    stage2(3)
    stage3(2)
    stage3(3)
    for i in range(ney):
        for k in range(4):
            to_p(i, k).wait_recv()
    lax.fori_loop(0, nex, gather, 0)

    rows = nex * ney * cap
    for k in range(edev):
        c_w(0, k).wait()
        c_w(1, k).wait()

        def ffn(f0, n):
            xk = xin[k].reshape(rows, d)
            g = _dot(xk, w1v[k, :, pl.ds(f0, n)])
            v = _dot(xk, w3v[k, :, pl.ds(f0, n)])
            act[k, :, pl.ds(f0, n)] = (jax.nn.silu(g) * v).astype(BF)

        def body(f, _):
            ffn(pl.multiple_of(f * fb, fb), fb)
            return 0
        lax.fori_loop(0, ff // fb, body, 0)
        if ff % fb:
            ffn(ff - ff % fb, ff % fb)

    slots = edev * ney * cap

    def r1(j, q):
        c = _xor(e, q, 3)
        return rcopy(O.at[j % 2, c], R.at[j, e], r1s.at[j % 2, q], r1r.at[j, q], (z, c))

    def r1w(j, q):
        c = _xor(e, q, 3)
        return rcopy(O.at[j % 2, c], R.at[j, c], r1s.at[j % 2, q], r1r.at[j, q], (z, c))

    def r2(j, i):
        s = zx(i)
        return rcopy(PS.at[j % 2, s], Q.at[j, z], r2s.at[j % 2, i], r2r.at[j, i], (s, e))

    def r2w(j, i):
        s = zx(i)
        return rcopy(PS.at[j % 2, s], Q.at[j, s], r2s.at[j % 2, i], r2r.at[j, i], (s, e))

    def step(j, _):
        @pl.when(j < nj)
        def _():
            c_w2(j, j % 2).wait()

            @pl.when(j >= 2)
            def _():
                for q in range(1, nex):
                    r1(j, q).wait_send()
            for k in range(edev):
                o = _dot(act[k], w2v[j % 2, k]).astype(BF)
                O[j % 2, :, k * ney * cap:(k + 1) * ney * cap, :] = o.reshape(nex, ney * cap, jc)

            @pl.when(j + 2 < nj)
            def _():
                c_w2(j + 2, j % 2).start()
            R[j, e] = O[j % 2, e]
            for q in range(1, nex):
                r1(j, q).start()

        @pl.when((j >= 1) & (j < nj + 1))
        def _():
            jj = j - 1

            @pl.when(jj >= 2)
            def _():
                for i in range(1, ney):
                    r2(jj, i).wait_send()
            for q in range(1, nex):
                r1w(jj, q).wait_recv()
            Rj = R[jj].reshape(nex * slots, jc)
            p = _dot(G[0], Rj) + _dot(G[1], Rj) + _dot(G[2], Rj)
            PS[jj % 2] = p.reshape(ney, C, jc)
            Q[jj, z] = PS[jj % 2, z]
            for i in range(1, ney):
                r2(jj, i).start()

        @pl.when(j >= 2)
        def _():
            jj = j - 2
            for i in range(1, ney):
                r2w(jj, i).wait_recv()
            q1, q2, q3 = _split3(Q[jj].reshape(ney * C, jc))
            bk = back[...]
            routed = _dot(bk, q1) + _dot(bk, q2) + _dot(bk, q3)
            cols = pl.ds(pl.multiple_of(jj * jc, jc), jc)
            y[:, cols] = (h[:, cols].astype(F32) + shr[:, cols] + routed).astype(BF)
        return 0

    lax.fori_loop(0, nj + 2, step, 0)

    for i in range(1, ney):
        zc[i].wait_send()
    for i in range(ney):
        for hf in (0, 1):
            to_x(i, hf).wait_send()
            to_y(i, hf).wait_send()
            to_d(i, hf).wait_send()
        for k in range(4):
            to_p(i, k).wait_send()
    for j in (nj - 2, nj - 1):
        for q in range(1, nex):
            r1(j, q).wait_send()
        for i in range(1, ney):
            r2(j, i).wait_send()


def _moe(xc, h, u, back, ws1, ws3, ws2, w1, w3, w2, ney, nex, C, cap):
    b, d = u.shape
    edev, _, ff = w1.shape
    nj, fb = 4, 256
    jc = d // nj
    rows = ney * cap
    vm = pl.BlockSpec(memory_space=VMEM)
    an = pl.BlockSpec(memory_space=ANY)
    DMA = pltpu.SemaphoreType.DMA
    ka, kb = 128, 176
    return pl.pallas_call(
        functools.partial(_moe_kernel, ney, nex, C, cap, nj, fb),
        out_shape=jax.ShapeDtypeStruct((b, d), BF),
        in_specs=[an, vm, vm, vm] + [an] * 6,
        out_specs=vm,
        scratch_shapes=[
            pltpu.VMEM((nex, ney, C, d + META), BF),
            pltpu.VMEM((edev, d, ff), BF), pltpu.VMEM((edev, d, ff), BF),
            pltpu.VMEM((2, edev, ff, jc), BF),
            pltpu.VMEM((2, 2, ka, ff), BF), pltpu.VMEM((2, kb, d), BF),
            pltpu.VMEM((edev, nex, rows, d), BF),
            pltpu.VMEM((edev, nex * rows, ff), BF),
            pltpu.VMEM((2, nex, edev * rows, jc), BF),
            pltpu.VMEM((nj, nex, edev * rows, jc), BF),
            pltpu.VMEM((2, ney, C, jc), F32),
            pltpu.VMEM((nj, ney, C, jc), F32),
            pltpu.VMEM((3, ney * C, nex * edev * rows), BF),
            pltpu.VMEM((2, b, ff), F32),
            pltpu.VMEM((b, d), F32),
            DMA, DMA((ney,)), DMA((ney,)),
            DMA((ney, 2)), DMA((ney, 2)), DMA((ney, 2)), DMA((ney, 2)), DMA((ney, 2)), DMA((ney, 2)),
            DMA((ney, 4)), DMA((ney, 4)),
            DMA((2, edev)), DMA((2,)), DMA((2, 2)), DMA((2,)),
            DMA((2, nex)), DMA((nj, nex)), DMA((2, ney)), DMA((nj, ney)),
        ],
        name='moe',
        compiler_params=pltpu.CompilerParams(vmem_limit_bytes=67043328, collective_id=0, has_side_effects=True),
    )(xc, h, u, back, ws1, ws3, ws2, w1, w3, w2)


def solution(mesh):
    ney, nex = mesh.shape['ey'], mesh.shape['ex']
    rows = P(('ey', 'ex'))
    rep = P()

    def local(x, kv_k, kv_v, lens, topk_idx, gates, ln1, ln2, wq, wo, ws1, ws3, ws2, w1, w3, w2):
        b = x.shape[0]
        k = topk_idx.shape[1]
        n_exp = w1.shape[0] * ney * nex
        cap = max(4, (2 * b * k + n_exp - 1) // n_exp)
        C = b
        h, u, xc, back = _attention(x, kv_k, kv_v, lens, topk_idx.T, gates.T, ln1, ln2, wq, wo, ney, n_exp, C, cap)
        return _moe(xc, h, u, back, ws1, ws3, ws2, w1, w3, w2, ney, nex, C, cap)

    return jax.shard_map(
        local, mesh=mesh,
        in_specs=(rows, rows, rows, rows, rows, rows, rep, rep, rep, rep, rep, rep, rep, rows, rows, rows),
        out_specs=rows, check_vma=False)
```

time: 252 us -> 156 us (0.62)
  Pallas kernels: 0 us -> 151 us
  blocking collectives: 69.2 us -> 0 us
  waiting for transfers between devices: 57.8 us -> 0 us
  matrix products: 50.2 us -> 0 us
  local copies, waits for them, and re-layouts: 38.3 us -> 4.24 us
  other arithmetic: 18.6 us -> 0 us
  between operations: 13.8 us -> 0.02 us
  starting transfers between devices: 3.82 us -> 0 us
    pallas_call x0 -> x2, Pallas kernels: none -> 151 us  [the longest x1 134 us: _moe(): pl.pallas_call(functools.partial(_moe_kernel, ney, nex, C, cap, nj, fb),...]
    dot_general x8 -> x0, matrix products: 46.7 us -> none  [the longest x1 10.1 us: _experts(): g = jnp.einsum('erd,edf->erf', xin, w1, preferred_element_type=F32)]
    all_to_all x1 -> x0, blocking collectives: 41.3 us -> none  [local(): recv = lax.all_to_all(send, 'ex', 0, 0)]
    reduce_scatter x1 -> x0, waiting for transfers between devices: 39.7 us -> none  [local(): lax.psum_scatter(partial[:ey * b].reshape(ey, b, d), 'ey', scatter_dimens...]
    all_gather x2 -> x0, blocking collectives: 27.8 us -> none  [the longest x1 14.8 us: local(): t_g = lax.all_gather(topk_idx, 'ey')]
    all_to_all x1 -> x0, waiting for transfers between devices: 18 us -> none  [local(): ret = lax.all_to_all(back, 'ex', 0, 0).reshape(nslotv, d)]
    gather x6 -> x0, local copies, waits for them, and re-layouts: 17.4 us -> none  [the longest x5 13.1 us: _ranks(): return jnp.take_along_axis(before, topk, axis=-1)]
    scatter-add x1 -> x0, other arithmetic: 15.4 us -> none  [local(): jnp.zeros((ey * b + 1, d), F32).at[slot_tok]]
  transfers between devices with their start and end apart: 3 -> 0, of which waited for: 2 -> 0; matrix products, arithmetic and copies ran while one was open for 12% -> 0% of each run, Pallas kernels for 0% -> 0%
where the time goes in v1:
time: 156 us
  Pallas kernels  151 us (97%)
  local copies, waits for them, and re-layouts  4.24 us (3%)
    pallas_call x1, Pallas kernels, _moe(): pl.pallas_call(functools.partial(_moe_kernel, ney, nex, C, cap, nj, fb),...  134 us
    pallas_call x1, Pallas kernels, _attention(): pl.pallas_call(functools.partial(_attn_kernel, nrow, n_exp, C, cap), out_...  17.3 us

profile of v1, /device:TPU:0, one launch (start us, length us, event | category | flops | bytes accessed | tf_op | source)
XLA Modules:
  0.0 155.6 jit_solution(12939391266040228815)
XLA Ops:
  0.0 1.3 reshape.12.ln1
  1.3 1.3 reshape.13.ln2
  2.6 17.3 %attention.1 = (bf16[64,2048]{1,0:T(8,128)(2,1)}, bf16[64,2048]{1,0:T(8,128)(2,1)}, bf16[4,64,2176]{2,1,0:T(8,128)(2,1)}, bf16[64,256]{1,0:T(8,128)(2,1)}) custom-call(s32[64]{0:T(128)} %lens.1, bf16[64,2048]{1,0:T(8,128)(2,1)} %x.1, s32[6,64]{1,0:T(8,128)} %bitcast.6, f32[6,64]{1,0:T(8,128)} %bitcast.7, bf16[1,2048]{1,0:T(2,128)(2,1)} %reshape.12.ln1, ...), custom_call_target="tpu_custom_call" | custom-call | tf_op jit(solution)/shard_map/attention/pallas_call | solution.py:157
  19.8 134.1 %moe.1 = bf16[64,2048]{1,0:T(8,128)(2,1)} custom-call(bf16[4,64,2176]{2,1,0:T(8,128)(2,1)} %get-tuple-element.9.xc, bf16[64,2048]{1,0:T(8,128)(2,1)} %get-tuple-element.10.h, bf16[64,2048]{1,0:T(8,128)(2,1)} %get-tuple-element.11.u, bf16[64,256]{1,0:T(8,128)(2,1)} %get-tuple-element.12.back, bf16[2048,1408]{1,0:T(8,128)(2,1)} %ws1.1, ...), custom_call_target="tpu_custom_call" | custom-call | tf_op jit(solution)/shard_map/moe/pallas_call | solution.py:487
  154.0 1.7 %copy.18 = bf16[64,2048]{1,0:T(8,128)(2,1)} copy(bf16[64,2048]{1,0:T(8,128)(2,1)} %moe.1) | data formatting | bytes 524288
